TPU v7x, 32 devices: a whole 2x2x4 slice. The times are simulated.
32 devices in a mesh: groups: 2 (over y), blk: 4 (over z), rep: 2 (over x), sub: 2 (over core).
Axes of the slice: x: 2, y: 2, z: 4, core: 2. Of those that a mesh axis runs over, the one named last changes fastest.
Arguments:
- replica_delta: bfloat16 [32, 32, 4608], P(('groups', 'blk', 'rep', 'sub')), parts along dimension 0, may hold values from -150 to 150
- momentum: float32 [64, 4608], P(('groups', 'blk')), parts along dimension 0, may hold values from -6 to 6
- params: float32 [64, 4608], P(('groups', 'blk')), parts along dimension 0, may hold values from -6 to 6
- prev_master: float32 [64, 4608], P(('groups', 'blk')), parts along dimension 0, may hold values from -6 to 6
Outputs:
- new_params: float32 [64, 4608], P(('groups', 'blk')), parts along dimension 0
- new_momentum: float32 [64, 4608], P(('groups', 'blk')), parts along dimension 0
- prev_weights: bfloat16 [64, 4608], P('groups'), parts along dimension 0
There are 2 independent parts, one for each index of `groups`. A program takes and returns all parts, laid end to end along the dimension named above; each array names one. Nothing has to cross between parts.
All inputs are finite; a program needn't handle non-finite values.
Results may differ from a plain program's by a relative error of at most 0.012.
Values may be sent and summed in bfloat16 or wider, within the bound.
No kernel may reach another device: no remote copies, remote signals or barrier semaphores. Data moves between devices by JAX's collectives and lax.ppermute only.
A program may use at most 64 MiB of HBM per device.

v0:
```python
import jax
import jax.numpy as jnp
from jax import lax
from jax.sharding import PartitionSpec as P

momentum_coef = 0.9
outer_rate = 0.7


def per_device(replica_delta, momentum, params, prev_master):
    own_delta = replica_delta[0]
    width = own_delta.shape[1]
    entries = own_delta.shape[0] * width
    share_sum = lax.psum_scatter(
        own_delta.astype(jnp.float32).astype(jnp.bfloat16), "blk", scatter_dimension=0, tiled=True
    )
    summed = lax.psum(share_sum, ("rep", "sub")).astype(jnp.float32)
    squares = lax.psum(jnp.sum(summed * summed), "blk")
    clip_factor = jnp.minimum(
        jnp.float32(1.0), jnp.sqrt(jnp.float32(entries)) / jnp.sqrt(squares + 1e-06)
    )
    scaled = clip_factor * summed
    new_momentum = momentum_coef * momentum + scaled
    new_params = params - outer_rate * (scaled + momentum_coef * new_momentum)
    prev_weights = lax.all_gather(prev_master.astype(jnp.bfloat16), "blk", axis=0, tiled=True)
    return (new_params, new_momentum, prev_weights)


def solution(mesh):
    in_specs = (
        P(("groups", "blk", "rep", "sub"), None, None),
        P(("groups", "blk"), None),
        P(("groups", "blk"), None),
        P(("groups", "blk"), None),
    )
    out_specs = (P(("groups", "blk"), None), P(("groups", "blk"), None), P("groups", None))
    return jax.shard_map(
        per_device, mesh=mesh, in_specs=in_specs, out_specs=out_specs, check_vma=False
    )
```

profile of v0, /device:TPU:0, one launch (start us, length us, event | category | flops | bytes accessed | tf_op | source)
XLA Modules:
  0.0 86.8 jit_solution(3447558341183904942)
XLA Ops:
  7.2 0.0 reduce-scatter.2.cloned.1.call-start
  7.2 0.0 copy-start.1
  7.2 0.7 reduce-scatter.2.cloned.1.call-update
  7.9 0.0 all-reduce.2.cloned.1.call-start
  7.9 0.2 copy-done.1
  8.1 25.1 %reduce-scatter.2.cloned.1.call-done = bf16[8,4608]{1,0:T(8,128)(2,1)} async-done(((bf16[32,4608]{1,0:T(8,128)(2,1)}), bf16[8,4608]{1,0:T(8,128)(2,1)}) %reduce-scatter.2.cloned.1.call-update) | async-done | bytes 73744 | tf_op jit(solution)/shard_map/reduce_scatter | solution.py:14
  33.2 0.0 all-reduce.2.cloned.1.call-update
  33.2 0.0 copy-start.2
  33.2 0.0 copy-start.3
  33.2 14.1 %all_gather.3 = bf16[32,4608]{1,0:T(8,128)(2,1)S(1)} all-gather(bf16[8,4608]{1,0:T(8,128)(2,1)S(1)} %convert_element_type.9), channel_id=1, replica_groups=mesh['groups'=2,'blk'=4,'rep'=2,'sub'=2] {'blk'}, dimensions={0}, use_global_device_ids=true | all-gather | bytes 368640 | tf_op jit(solution)/shard_map/all_gather | solution.py:25
  47.4 16.1 %all-reduce.2.cloned.1.call-done = bf16[8,4608]{1,0:T(8,128)(2,1)} async-done(((bf16[8,4608]{1,0:T(8,128)(2,1)}), bf16[8,4608]{1,0:T(8,128)(2,1)}) %all-reduce.2.cloned.1.call-update) | async-done | bytes 73744 | tf_op jit(solution)/shard_map/psum | solution.py:17
  63.5 0.0 copy-start
  63.5 1.6 %fusion.4 = f32[]{:T(128)} fusion(bf16[8,4608]{1,0:T(8,128)(2,1)} %all-reduce.2.cloned.1.call-done), kind=kLoop, calls=%fused_computation.6 | loop fusion | flops 110591 | bytes 73732 | tf_op jit(solution)/shard_map/reduce_sum | solution.py:18
  65.1 12.7 %psum.15 = f32[]{:T(128)} all-reduce(f32[]{:T(128)} %fusion.4), channel_id=1, replica_groups=mesh['groups'=2,'blk'=4,'rep'=2,'sub'=2] {'blk'}, use_global_device_ids=true, to_apply=%region_3.0 | all-reduce | flops 1 | bytes 8 | tf_op jit(solution)/shard_map/psum | solution.py:18
  78.4 0.0 copy-done.2
  78.5 0.0 copy-done.3
  78.5 0.0 copy-done
  78.5 0.8 fusion.3
  79.2 0.7 copy.9
  (1 shorter events, 0.0 us)
Async XLA Ops:
  7.2 26.0 %reduce-scatter.2.cloned.1.call-start = ((), (), s32[]{:S(2)}) async-start(), calls=%async_computation.1 | async-start | bytes 368640 | tf_op jit(solution)/shard_map/reduce_scatter | solution.py:14
  7.2 0.9 %copy-start.1 = (f32[8,4608]{1,0:T(8,128)S(1)}, f32[8,4608]{1,0:T(8,128)}, u32[]{:S(2)}) copy-start(f32[8,4608]{1,0:T(8,128)} %param.7) | copy-start | bytes 442372
  7.9 55.6 %all-reduce.2.cloned.1.call-start = ((), (), s32[]{:S(2)}) async-start(), calls=%async_computation.2 | async-start | bytes 147456 | tf_op jit(solution)/shard_map/psum | solution.py:17
  33.2 45.2 %copy-start.2 = (f32[8,4608]{1,0:T(8,128)S(1)}, f32[8,4608]{1,0:T(8,128)}, u32[]{:S(2)}) copy-start(f32[8,4608]{1,0:T(8,128)} %param.6) | copy-start | bytes 442372
  33.2 45.2 %copy-start.3 = (f32[8,4608]{1,0:T(8,128)S(1)}, f32[8,4608]{1,0:T(8,128)}, u32[]{:S(2)}) copy-start(f32[8,4608]{1,0:T(8,128)} %param.5) | copy-start | bytes 442372
  63.5 15.0 %copy-start = (bf16[8,4608]{1,0:T(8,128)(2,1)S(1)}, bf16[8,4608]{1,0:T(8,128)(2,1)}, u32[]{:S(2)}) copy-start(bf16[8,4608]{1,0:T(8,128)(2,1)} %all-reduce.2.cloned.1.call-done) | copy-start | bytes 221188
Sparse Core Ops, SparseCore 0:
  10.2 22.9 reduce-scatter.1
  35.5 27.9 all-reduce.1
where the time goes:
time: 87 us; the launch traced here: 86.8 us
  waiting for transfers between devices  41.9 us (48%)
  blocking collectives  26.8 us (31%)
  between operations  14.8 us (17%)
  other arithmetic  2.36 us (3%)
  local copies, waits for them, and re-layouts  0.91 us (1%)
    reduce_scatter x1, waiting for transfers between devices, per_device(): lax.psum_scatter(own_delta.astype(jnp.float32).astype(jnp.bfloat16), 'blk...  25.1 us
    psum x1, waiting for transfers between devices, per_device(): summed = lax.psum(share_sum, ('rep', 'sub')).astype(jnp.float32)  16.1 us
    all_gather x1, blocking collectives, per_device(): lax.all_gather(prev_master.astype(jnp.bfloat16), 'blk', axis=0, tiled=True)  14.1 us
    psum x1, blocking collectives, per_device(): squares = lax.psum(jnp.sum(summed * summed), 'blk')  12.7 us
  transfers between devices with their start and end apart: 2, of which 2 were waited for; matrix products, arithmetic and copies ran while one was open for 0% of the time, Pallas kernels for 0%

commit v1 on v0

--- a/solution.py
+++ b/solution.py
@@ -14,7 +14,10 @@
     share_sum = lax.psum_scatter(
         own_delta.astype(jnp.float32).astype(jnp.bfloat16), "blk", scatter_dimension=0, tiled=True
     )
-    summed = lax.psum(share_sum, ("rep", "sub")).astype(jnp.float32)
+    follow_the_ranges = lambda mat, ax_name, a_name: jax.lax.psum(
+        jax.lax.psum(mat, ax_name), a_name
+    )
+    summed = follow_the_ranges(share_sum, "sub", "rep").astype(jnp.float32)
     squares = lax.psum(jnp.sum(summed * summed), "blk")
     clip_factor = jnp.minimum(
         jnp.float32(1.0), jnp.sqrt(jnp.float32(entries)) / jnp.sqrt(squares + 1e-06)

time: 87 us -> 98.8 us (1.14)
  waiting for transfers between devices: 41.9 us -> 53.9 us
    psum x1 -> x2, waiting for transfers between devices: 16.1 us -> 28 us  [the longest x1 18.2 us: per_device(): jax.lax.psum(mat, ax_name)]
  transfers between devices with their start and end apart: 2 -> 3, of which waited for: 2 -> 3; matrix products, arithmetic and copies ran while one was open for 0% -> 0% of each run, Pallas kernels for 0% -> 0%
where the time goes in v1:
time: 98.8 us; the launch traced here: 98.6 us
  waiting for transfers between devices  53.9 us (55%)
  blocking collectives  26.9 us (27%)
  between operations  14.5 us (15%)
  other arithmetic  2.36 us (2%)
    reduce_scatter x1, waiting for transfers between devices, per_device(): lax.psum_scatter(own_delta.astype(jnp.float32).astype(jnp.bfloat16), 'blk...  25.3 us
    psum x1, waiting for transfers between devices, per_device(): jax.lax.psum(mat, ax_name)  18.2 us
    all_gather x1, blocking collectives, per_device(): lax.all_gather(prev_master.astype(jnp.bfloat16), 'blk', axis=0, tiled=True)  14.6 us
    psum x1, blocking collectives, per_device(): squares = lax.psum(jnp.sum(summed * summed), 'blk')  12.3 us
    psum x1, waiting for transfers between devices, per_device(): jax.lax.psum(jax.lax.psum(mat, ax_name), a_name)  9.81 us
  transfers between devices with their start and end apart: 3, of which 3 were waited for; matrix products, arithmetic and copies ran while one was open for 0% of the time, Pallas kernels for 0%

profile of v1, /device:TPU:0, one launch (start us, length us, event | category | flops | bytes accessed | tf_op | source)
XLA Modules:
  0.0 98.6 jit_solution(16130087390763525409)
XLA Ops:
  7.2 0.0 reduce-scatter.2.cloned.1.call-start
  7.2 0.0 copy-start.1
  7.2 0.7 reduce-scatter.2.cloned.1.call-update
  7.9 0.0 all-reduce.3.cloned.1.call-start
  7.9 25.3 %reduce-scatter.2.cloned.1.call-done = bf16[8,4608]{1,0:T(8,128)(2,1)} async-done(((bf16[32,4608]{1,0:T(8,128)(2,1)}), bf16[8,4608]{1,0:T(8,128)(2,1)}) %reduce-scatter.2.cloned.1.call-update) | async-done | bytes 73744 | tf_op jit(solution)/shard_map/reduce_scatter | solution.py:14
  33.2 0.0 all-reduce.3.cloned.1.call-update
  33.2 0.0 all-reduce.5.cloned.1.call-start
  33.3 0.0 copy-done.1
  33.3 18.2 %all-reduce.3.cloned.1.call-done = bf16[8,4608]{1,0:T(8,128)(2,1)} async-done(((bf16[8,4608]{1,0:T(8,128)(2,1)}), bf16[8,4608]{1,0:T(8,128)(2,1)}) %all-reduce.3.cloned.1.call-update) | async-done | bytes 73744 | tf_op jit(solution)/shard_map/psum | solution.py:18
  51.5 0.0 all-reduce.5.cloned.1.call-update
  51.5 0.0 copy-start.2
  51.5 0.0 copy-start.3
  51.5 14.6 %all_gather.3 = bf16[32,4608]{1,0:T(8,128)(2,1)S(1)} all-gather(bf16[8,4608]{1,0:T(8,128)(2,1)S(1)} %convert_element_type.9), channel_id=1, replica_groups=mesh['groups'=2,'blk'=4,'rep'=2,'sub'=2] {'blk'}, dimensions={0}, use_global_device_ids=true | all-gather | bytes 368640 | tf_op jit(solution)/shard_map/all_gather | solution.py:28
  66.1 9.8 %all-reduce.5.cloned.1.call-done = bf16[8,4608]{1,0:T(8,128)(2,1)} async-done(((bf16[8,4608]{1,0:T(8,128)(2,1)}), bf16[8,4608]{1,0:T(8,128)(2,1)}) %all-reduce.5.cloned.1.call-update) | async-done | bytes 73744 | tf_op jit(solution)/shard_map/psum | solution.py:17
  75.9 0.0 copy-start
  75.9 1.6 %fusion.4 = f32[]{:T(128)} fusion(bf16[8,4608]{1,0:T(8,128)(2,1)} %all-reduce.5.cloned.1.call-done), kind=kLoop, calls=%fused_computation.6 | loop fusion | flops 110591 | bytes 73732 | tf_op jit(solution)/shard_map/reduce_sum | solution.py:21
  77.5 12.3 %psum.23 = f32[]{:T(128)} all-reduce(f32[]{:T(128)} %fusion.4), channel_id=1, replica_groups=mesh['groups'=2,'blk'=4,'rep'=2,'sub'=2] {'blk'}, use_global_device_ids=true, to_apply=%region_4.0 | all-reduce | flops 1 | bytes 8 | tf_op jit(solution)/shard_map/psum | solution.py:21
  90.5 0.0 copy-done.2
  90.5 0.0 copy-done.3
  90.6 0.0 copy-done
  90.6 0.8 fusion.3
  91.3 0.7 copy.10
  (1 shorter events, 0.0 us)
Async XLA Ops:
  7.2 26.0 %reduce-scatter.2.cloned.1.call-start = ((), (), s32[]{:S(2)}) async-start(), calls=%async_computation.1 | async-start | bytes 368640 | tf_op jit(solution)/shard_map/reduce_scatter | solution.py:14
  7.2 26.1 %copy-start.1 = (f32[8,4608]{1,0:T(8,128)S(1)}, f32[8,4608]{1,0:T(8,128)}, u32[]{:S(2)}) copy-start(f32[8,4608]{1,0:T(8,128)} %param.7) | copy-start | bytes 442372
  7.9 43.6 %all-reduce.3.cloned.1.call-start = ((), (), s32[]{:S(2)}) async-start(), calls=%async_computation.2 | async-start | bytes 147456 | tf_op jit(solution)/shard_map/psum | solution.py:18
  33.2 42.7 %all-reduce.5.cloned.1.call-start = ((), (), s32[]{:S(2)}) async-start(), calls=%async_computation.3 | async-start | bytes 147456 | tf_op jit(solution)/shard_map/psum | solution.py:17
  51.5 39.0 %copy-start.2 = (f32[8,4608]{1,0:T(8,128)S(1)}, f32[8,4608]{1,0:T(8,128)}, u32[]{:S(2)}) copy-start(f32[8,4608]{1,0:T(8,128)} %param.6) | copy-start | bytes 442372
  51.5 39.0 %copy-start.3 = (f32[8,4608]{1,0:T(8,128)S(1)}, f32[8,4608]{1,0:T(8,128)}, u32[]{:S(2)}) copy-start(f32[8,4608]{1,0:T(8,128)} %param.5) | copy-start | bytes 442372
  75.9 14.6 %copy-start = (bf16[8,4608]{1,0:T(8,128)(2,1)S(1)}, bf16[8,4608]{1,0:T(8,128)(2,1)}, u32[]{:S(2)}) copy-start(bf16[8,4608]{1,0:T(8,128)(2,1)} %all-reduce.5.cloned.1.call-done) | copy-start | bytes 221188
Sparse Core Ops, SparseCore 0:
  10.2 22.9 reduce-scatter.1
  35.5 15.9 all-reduce.2
  53.7 22.1 all-reduce.4
